TPU v7x, 1024 devices: a whole 4x8x16 slice. The times are simulated.
1024 devices in a mesh: row: 32 (over y_lo, z), col: 32 (over x, y_hi, core).
Axes of the slice: x: 4, y: 8 (y_hi: 4, y_lo: 2; y = y_hi * 2 + y_lo), z: 16, core: 2. Of those that a mesh axis runs over, the one named last changes fastest.
Arguments:
- hidden: bfloat16 [2048, 4096], P('row'), may hold values from -6 to 6
- queries: bfloat16 [2048, 64, 128], P(('row', 'col')), may hold values from -6 to 6
- keys: bfloat16 [2048, 4, 64, 128], P(('row', 'col')), may hold values from -6 to 6
- values: bfloat16 [2048, 4, 64, 128], P(('row', 'col')), may hold values from -12 to 12
- out_proj: bfloat16 [8192, 4096], P('col'), may hold values from -0.0625 to 0.0625
- norm_gain: float32 [4096], replicated, may hold values from 0.4 to 1.6
- routes: int32 [2048, 8], P('row'), may hold values from 0 to 127, all different within a row; in each aligned block of 64 rows (0 to 63, 64 to 127, ...) at most 8 rows name the same one
- route_probs: float32 [2048, 8], P('row'), may hold values from 0.05 to 1
- w_gate: bfloat16 [4096, 131072], P(None, ('row', 'col')), may hold values from -0.09375 to 0.09375
- w_up: bfloat16 [4096, 131072], P(None, ('row', 'col')), may hold values from -0.09375 to 0.09375
- w_down: bfloat16 [131072, 4096], P(('row', 'col')), may hold values from -0.1875 to 0.1875
Outputs:
- updated: bfloat16 [2048, 4096], P(('row', 'col'))
Inputs may be any that keep to these rules, and one draw needn't show every extreme that they name: `routes`: each row names 8 different experts. In each aligned block of 64 rows (the requests of one index of row) no expert is named by more than 8 rows.
All inputs are finite; a program needn't handle non-finite values.
Results may differ from a plain program's by a relative error of at most 0.017.
Values may be sent and summed in bfloat16 or wider, within the bound.
No kernel may reach another device: no remote copies, remote signals or barrier semaphores. Data moves between devices by JAX's collectives and lax.ppermute only.
A program may use at most 32 MiB of HBM per device.

v0:
```python
import math

import jax
import jax.numpy as jnp
from jax import lax
from jax.experimental import pallas as pl
from jax.experimental.pallas import tpu as pltpu
from jax.sharding import Mesh, PartitionSpec as P

CAP = 8
NX, NY, NC = 4, 4, 2
COL = ("x", "yhi", "core")
F32 = jnp.float32
BF16 = jnp.bfloat16


def exchange(value, axis):
    return lax.all_to_all(value, axis, 0, 0, tiled=True)


def swap_cores(value):
    return lax.ppermute(value, "core", [(i, (i + 1) % NC) for i in range(NC)])


def turn(value, step):
    return lax.ppermute(value, "yhi", [(i, (i + step) % NY) for i in range(NY)])


def to_all(value, axis, length):
    return exchange(jnp.broadcast_to(value[None], (length, *value.shape)), axis)


def attention(queries, keys, values):
    tok, heads, hd = queries.shape
    kv = keys.shape[1]
    grouped = queries.reshape(tok, kv, heads // kv, hd)
    scores = jnp.einsum(
        "tgqd,tgpd->tgqp", grouped, keys, preferred_element_type=F32
    ) / math.sqrt(hd)
    attn_weights = jax.nn.softmax(scores, axis=-1).astype(BF16)
    context = jnp.einsum("tgqp,tgpd->tgqd", attn_weights, values, preferred_element_type=F32)
    return context.astype(BF16).reshape(tok, heads * hd)


def hidden_units(place_ref, own_ref, other_ref, gain_ref, wg_ref, wu_ref, act_ref):
    pieces, count, wide = own_ref.shape
    step = 2 * wide
    steps = pieces // 2
    total = jnp.zeros((count, 2 * wg_ref.shape[1]), F32)
    squares = jnp.zeros((count, step), F32)
    for flip, ref in enumerate((own_ref, other_ref)):
        first = ((place_ref[0] + flip) % NC) * steps
        for p in range(steps):
            rows = jnp.concatenate([ref[2 * p], ref[2 * p + 1]], axis=1).astype(F32)
            squares = squares + rows * rows
            scaled = (rows * gain_ref[pl.ds(first + p, 1), :]).astype(BF16)
            at = pl.multiple_of((first + p) * step, step)
            both = jnp.concatenate([wg_ref[pl.ds(at, step), :], wu_ref[pl.ds(at, step), :]], axis=1)
            total = total + jnp.dot(scaled, both, preferred_element_type=F32)
    features = 2 * steps * step
    inv = lax.rsqrt(jnp.sum(squares, axis=1, keepdims=True) / features + 1e-06)
    gate = total[:, : wg_ref.shape[1]] * inv
    up = total[:, wg_ref.shape[1] :] * inv
    act_ref[...] = (gate / (1.0 + jnp.exp(-gate)) * up).astype(BF16)


def down_rows(place_ref, own_ref, other_ref, wd0_ref, wd1_ref, wd2_ref, wd3_ref, out_ref):
    total = jnp.zeros(out_ref.shape, F32)
    for step, wd_ref in enumerate((wd0_ref, wd1_ref, wd2_ref, wd3_ref)):
        y = (place_ref[1] + NY - step) % NY
        for flip, ref in enumerate((own_ref, other_ref)):
            total = total + jnp.dot(ref[y], wd_ref[flip], preferred_element_type=F32)
    out_ref[...] = total.astype(BF16)


def project(h_ref, w_ref, out_ref):
    cols, _, thin = out_ref.shape
    half = cols // NC
    for core in range(NC):
        for p in range(0, half, 2):
            at = (core * half + p) * thin
            both = jnp.dot(
                h_ref[...], w_ref[:, at : at + 2 * thin], preferred_element_type=F32
            ).astype(BF16)
            out_ref[p * NC + core] = both[:, :thin]
            out_ref[(p + 1) * NC + core] = both[:, thin:]


def cut_features(place_ref, w_ref, same_ref, other_ref):
    thin = same_ref.shape[2] // NX
    for flip, ref in enumerate((same_ref, other_ref)):
        core = (place_ref[0] + flip) % NC
        for step in range(NY):
            y = (place_ref[1] + step) % NY
            for x in range(NX):
                at = pl.multiple_of(((core * NX + x) * NY + y) * thin, thin)
                ref[step, :, x * thin : (x + 1) * thin] = w_ref[:, pl.ds(at, thin)]


def spread(in_ref, out_ref):
    rows, slots, thin = in_ref.shape
    per = slots // NX
    for x in range(NX):
        piece = in_ref[:, x * per : (x + 1) * per, :].reshape(rows * per, thin)
        for y in range(NY):
            out_ref[x * NY + y] = piece


def local_call(body, outs, n_in, scalars=False):
    vmem = pl.BlockSpec(memory_space=pltpu.VMEM)
    head = [pl.BlockSpec(memory_space=pltpu.SMEM)] if scalars else []
    out_shape = [jax.ShapeDtypeStruct(shape, BF16) for shape in outs]
    single = len(outs) == 1
    return pl.pallas_call(
        body,
        out_shape=out_shape[0] if single else out_shape,
        in_specs=head + [vmem] * n_in,
        out_specs=vmem if single else [vmem] * len(outs),
        compiler_params=pltpu.CompilerParams(vmem_limit_bytes=24 * 1024 * 1024),
    )


def shards(
    hidden, queries, keys, values, out_proj, norm_gain, routes, route_probs, w_gate, w_up, w_down
):
    rows = lax.axis_size("row")
    x, yhi, core = lax.axis_index("x"), lax.axis_index("yhi"), lax.axis_index("core")
    col_id = (x * NY + yhi) * NC + core
    tok_dev = queries.shape[0]
    block, d_model = hidden.shape
    cols = NX * NY * NC
    thin = d_model // cols
    wide = d_model // (NY * NC)
    count = rows * CAP
    place_at = jnp.stack([core, yhi]).astype(jnp.int32)

    route_weight = (route_probs / jnp.sum(route_probs, axis=-1, keepdims=True)).astype(BF16)
    earlier = (jnp.arange(block)[:, None] < jnp.arange(block)[None, :]).astype(BF16)
    slots = jnp.arange(CAP, dtype=F32)

    def slotted(experts):
        match = routes.T[None, :, :] == experts[:, None, None]
        hits = jnp.any(match, axis=1)
        before = jnp.dot(hits.astype(BF16), earlier, preferred_element_type=F32)
        place = hits[:, None, :] & (before[:, None, :] == slots[None, :, None])
        return match, place.astype(BF16)

    _, place = slotted(jnp.arange(rows * NX, dtype=jnp.int32))
    place = place.reshape(rows * NX * CAP, block)
    match, mine = slotted(jnp.arange(rows, dtype=jnp.int32) * NX + x)
    chosen = jnp.sum(jnp.where(match, route_weight.T[None], jnp.zeros((), BF16)), axis=1)
    combine = (mine * chosen[:, None, :]).reshape(count, block).T

    context = attention(queries, keys, values)
    heads_out = jnp.moveaxis(context.reshape(tok_dev, cols, -1), 1, 0)
    head_rows = exchange(heads_out, COL).reshape(block, -1)

    part = local_call(project, [(cols, block, thin)], 2)(head_rows, out_proj)
    attn = jnp.sum(exchange(part, COL).astype(F32), axis=0)
    own_at = ((core * NX + x) * NY + yhi) * thin
    resid = lax.dynamic_slice_in_dim(hidden, own_at, thin, 1).astype(F32) + attn

    outgoing = jnp.dot(place, resid.astype(BF16), preferred_element_type=F32).astype(BF16)
    arrived = exchange(outgoing.reshape(rows, NX * CAP, thin), "row")

    hid = w_down.shape[0]
    same, rest = local_call(cut_features, [(NY, hid, wide)] * 2, 1, True)(place_at, w_down)
    pieces = [jnp.stack(pair) for pair in zip(same, swap_cores(rest))]
    down = [pieces[0]] + [turn(pieces[step], step) for step in (1, 3, 2)]
    down = [down[0], down[1], down[3], down[2]]

    by_expert = local_call(spread, [(NX * NY, count, thin)], 1)(arrived)
    own = exchange(by_expert, ("x", "yhi"))
    other = swap_cores(own)

    act = local_call(hidden_units, [(count, w_gate.shape[1])], 5, True)(
        place_at, own, other, norm_gain.reshape(-1, 2 * thin), w_gate, w_up
    )
    own_act = to_all(act, "yhi", NY)
    other_act = swap_cores(own_act)
    back = local_call(down_rows, [(count, wide)], 6, True)(place_at, own_act, other_act, *down)
    returned = exchange(back.reshape(rows, CAP, wide), "row").reshape(count, wide)

    attn_here = jnp.concatenate([jnp.where(x == i, attn, 0.0) for i in range(NX)], axis=1)
    mixed = jnp.dot(combine, returned, preferred_element_type=F32) + attn_here
    final = exchange(mixed.astype(BF16).reshape(cols, tok_dev, wide), COL)
    final = jnp.sum(final.astype(F32).reshape(NX, NY, NC, tok_dev, NX, thin), axis=0)
    final = jnp.transpose(final, (2, 1, 3, 0, 4)).reshape(tok_dev, d_model)
    own_hidden = lax.dynamic_slice_in_dim(hidden, col_id * tok_dev, tok_dev, 0)
    return (own_hidden.astype(F32) + final).astype(BF16)


def solution(mesh):
    rows = mesh.shape["row"]
    fine = Mesh(mesh.devices.reshape(rows, NX, NY, NC), ("row",) + COL)
    every = ("row",) + COL
    return jax.shard_map(
        shards,
        mesh=fine,
        in_specs=(
            P("row", None),
            P(every, None, None),
            P(every, None, None, None),
            P(every, None, None, None),
            P(COL, None),
            P(),
            P("row", None),
            P("row", None),
            P(None, every),
            P(None, every),
            P(every, None),
        ),
        out_specs=P(every, None),
        check_vma=False,
    )
```

profile of v0, /device:TPU:1, one launch (start us, length us, event | category | flops | bytes accessed | tf_op | source)
XLA Modules:
  0.0 221.5 jit_solution(10659873750672172175)
XLA Ops:
  0.0 1.1 convolution_multiply_fusion
  1.1 0.2 fusion.31
  1.4 0.3 convolution_convert_fusion.1
  1.7 26.5 %all_to_all.35 = bf16[32,2,256]{2,1,0:T(2,128)(2,1)S(1)} all-to-all(bf16[32,2,256]{2,1,0:T(2,128)(2,1)S(1)} %bitcast.39), channel_id=1, replica_groups=mesh['row'=32,'x'=4,'yhi'=4,'core'=2] {'x','yhi','core'}, dimensions={0} | all-to-all | bytes 65536 | tf_op jit(solution)/shard_map/all_to_all | solution.py:18
  28.3 1.6 copy-done.1
  29.8 1.3 shard_map.109
  31.1 3.9 %all-to-all-start.1 = ((bf16[32,64,128]{2,1,0:T(8,128)(2,1)}), bf16[32,64,128]{2,1,0:T(8,128)(2,1)S(1)}, u32[]{:S(2)}, u32[]{:S(2)}) async-start(bf16[32,64,128]{2,1,0:T(8,128)(2,1)} %shard_map.109), calls=%async_computation.1 | async-start | bytes 1048576 | tf_op jit(solution)/shard_map/all_to_all | solution.py:18
  35.1 0.1 fusion.11
  35.2 0.1 copy.25
  35.4 0.1 eq.83
  35.5 0.2 fusion.22
  35.7 15.6 %all-to-all-done.1 = bf16[32,64,128]{2,1,0:T(8,128)(2,1)S(1)} async-done(((bf16[32,64,128]{2,1,0:T(8,128)(2,1)}), bf16[32,64,128]{2,1,0:T(8,128)(2,1)S(1)}, u32[]{:S(2)}, u32[]{:S(2)}) %all-to-all-start.1) | async-done | bytes 524320 | tf_op jit(solution)/shard_map/all_to_all | solution.py:18
  51.3 0.1 convert_reduce_fusion
  51.4 1.1 convolution_convert_fusion
  52.5 34.6 %all_to_all.36.in_ref = bf16[32,32,128]{2,1,0:T(8,128)(2,1)S(1)} all-to-all(bf16[32,32,128]{2,1,0:T(8,128)(2,1)S(1)} %bitcast.37), channel_id=1, replica_groups=mesh['row'=32,'x'=4,'yhi'=4,'core'=2] {'row'}, dimensions={0} | all-to-all | bytes 524288 | tf_op jit(solution)/shard_map/all_to_all | solution.py:18
  87.1 0.1 shard_map.110
  87.3 0.0 copy-start.2
  87.3 0.0 copy-start.3
  87.3 32.9 %all_to_all.37.own_ref = bf16[16,256,128]{2,1,0:T(8,128)(2,1)S(1)} all-to-all(bf16[16,256,128]{2,1,0:T(8,128)(2,1)S(1)} %shard_map.110), channel_id=1, replica_groups=mesh['row'=32,'x'=4,'yhi'=4,'core'=2] {'x','yhi'}, dimensions={0} | all-to-all | bytes 2097152 | tf_op jit(solution)/shard_map/all_to_all | solution.py:18
  120.3 4.5 %collective-permute-start = (bf16[16,256,128]{2,1,0:T(8,128)(2,1)S(1)}, bf16[16,256,128]{2,1,0:T(8,128)(2,1)}, u32[]{:S(2)}, u32[]{:S(2)}) collective-permute-start(bf16[16,256,128]{2,1,0:T(8,128)(2,1)S(1)} %all_to_all.37.own_ref), channel_id=1, source_target_pairs={{0,1},{1,0},{2,3},{3,2},{4,5},{5,4},{6,7},{7,6},{8,9},{9,8},{10,11... | collective-permute-start | bytes 3145736 | tf_op jit(solution)/shard_map/ppermute | solution.py:22
  124.8 0.1 pad_add_fusion.place_ref
  124.9 1.6 shard_map.112
  126.5 0.8 copy-done.5
  127.3 1.9 collective-permute-start.2
  129.2 1.9 fusion.29
  131.1 2.1 shard_map.111
  133.2 0.7 broadcast_in_dim.22
  133.9 3.4 %all-to-all-start.4 = ((bf16[4,256,128]{2,1,0:T(8,128)(2,1)}), bf16[4,256,128]{2,1,0:T(8,128)(2,1)S(1)}, u32[]{:S(2)}, u32[]{:S(2)}) async-start(bf16[4,256,128]{2,1,0:T(8,128)(2,1)} %broadcast_in_dim.22), calls=%async_computation.4 | async-start | bytes 524288 | tf_op jit(solution)/shard_map/all_to_all | solution.py:18
  137.3 1.1 fusion.30
  138.5 0.9 pad_maximum_fusion.1
  139.4 4.2 %collective-permute-start.3 = (bf16[2,128,512]{2,1,0:T(8,128)(2,1)S(1)}, bf16[2,128,512]{2,1,0:T(8,128)(2,1)S(1)}, u32[]{:S(2)}, u32[]{:S(2)}) collective-permute-start(bf16[2,128,512]{2,1,0:T(8,128)(2,1)S(1)} %pad_maximum_fusion.1), channel_id=1, source_target_pairs={{0,2},{2,4},{4,6},{6,0},{1,3},{3,5},{5,7},{7,1},{8,10},{10,12},{12... | collective-permute-start | bytes 786440 | tf_op jit(solution)/shard_map/ppermute | solution.py:26
  143.7 5.2 %collective-permute-start.4 = (bf16[2,128,512]{2,1,0:T(8,128)(2,1)S(1)}, bf16[2,128,512]{2,1,0:T(8,128)(2,1)S(1)}, u32[]{:S(2)}, u32[]{:S(2)}) collective-permute-start(bf16[2,128,512]{2,1,0:T(8,128)(2,1)S(1)} %pad_maximum_fusion.2), channel_id=1, source_target_pairs={{0,4},{2,6},{4,0},{6,2},{1,5},{3,7},{5,1},{7,3},{8,12},{10,14},{12... | collective-permute-start | bytes 786440 | tf_op jit(solution)/shard_map/ppermute | solution.py:26
  148.9 5.2 %collective-permute-start.5 = (bf16[2,128,512]{2,1,0:T(8,128)(2,1)S(1)}, bf16[2,128,512]{2,1,0:T(8,128)(2,1)S(1)}, u32[]{:S(2)}, u32[]{:S(2)}) collective-permute-start(bf16[2,128,512]{2,1,0:T(8,128)(2,1)S(1)} %pad_maximum_fusion.3), channel_id=1, source_target_pairs={{0,6},{2,0},{4,2},{6,4},{1,7},{3,1},{5,3},{7,5},{8,14},{10,8},{12,... | collective-permute-start | bytes 786440 | tf_op jit(solution)/shard_map/ppermute | solution.py:26
  154.2 3.5 %collective-permute-start.1 = (bf16[4,256,128]{2,1,0:T(8,128)(2,1)S(1)}, bf16[4,256,128]{2,1,0:T(8,128)(2,1)S(1)}, u32[]{:S(2)}, u32[]{:S(2)}) collective-permute-start(bf16[4,256,128]{2,1,0:T(8,128)(2,1)S(1)} %all-to-all-done.4.own_ref), channel_id=1, source_target_pairs={{0,1},{1,0},{2,3},{3,2},{4,5},{5,4},{6,7},{7,6},{8,9},{9,8},{10,11... | collective-permute-start | bytes 786440 | tf_op jit(solution)/shard_map/ppermute | solution.py:22
  157.8 9.3 %collective-permute-done.4.wd2_ref = bf16[2,128,512]{2,1,0:T(8,128)(2,1)S(1)} collective-permute-done((bf16[2,128,512]{2,1,0:T(8,128)(2,1)S(1)}, bf16[2,128,512]{2,1,0:T(8,128)(2,1)S(1)}, u32[]{:S(2)}, u32[]{:S(2)}) %collective-permute-start.4) | collective-permute-done | bytes 262176 | tf_op jit(solution)/shard_map/ppermute | solution.py:26
  167.1 1.8 collective-permute-done.5.wd3_ref
  168.9 1.9 shard_map.113
  170.8 8.3 %all-to-all-start.5 = ((bf16[32,8,512]{2,1,0:T(8,128)(2,1)}), bf16[32,8,512]{2,1,0:T(8,128)(2,1)S(1)}, u32[]{:S(2)}, u32[]{:S(2)}) async-start(bf16[32,8,512]{2,1,0:T(8,128)(2,1)} %bitcast.9), calls=%async_computation.5 | async-start | bytes 524288 | tf_op jit(solution)/shard_map/all_to_all | solution.py:18
  179.1 0.1 compare_reduce_fusion
  179.2 0.1 fusion.16
  179.3 0.1 fusion.23
  179.5 19.8 %all-to-all-done.5 = bf16[32,8,512]{2,1,0:T(8,128)(2,1)S(1)} async-done(((bf16[32,8,512]{2,1,0:T(8,128)(2,1)}), bf16[32,8,512]{2,1,0:T(8,128)(2,1)S(1)}, u32[]{:S(2)}, u32[]{:S(2)}) %all-to-all-start.5) | async-done | bytes 262176 | tf_op jit(solution)/shard_map/all_to_all | solution.py:18
  199.3 0.2 fusion.2
  199.5 0.7 reshape.54
  200.2 9.9 %all-to-all-start.6 = ((bf16[32,2,512]{2,1,0:T(2,128)(2,1)}), bf16[32,2,512]{2,1,0:T(2,128)(2,1)S(1)}, u32[]{:S(2)}, u32[]{:S(2)}) async-start(bf16[32,2,512]{2,1,0:T(2,128)(2,1)} %reshape.54), calls=%async_computation.6 | async-start | bytes 131072 | tf_op jit(solution)/shard_map/all_to_all | solution.py:18
  210.1 9.7 %all-to-all-done.6 = bf16[32,2,512]{2,1,0:T(2,128)(2,1)S(1)} async-done(((bf16[32,2,512]{2,1,0:T(2,128)(2,1)}), bf16[32,2,512]{2,1,0:T(2,128)(2,1)S(1)}, u32[]{:S(2)}, u32[]{:S(2)}) %all-to-all-start.6) | async-done | bytes 65568 | tf_op jit(solution)/shard_map/all_to_all | solution.py:18
  219.8 0.1 reshape.59
  220.0 1.5 add_convert_fusion
  (38 shorter events, 0.4 us)
Async XLA Ops:
  0.0 1.3 copy-start
  1.3 33.7 %copy-start.8 = (s32[64,8]{0,1:T(8,128)S(1)}, s32[64,8]{0,1:T(8,128)}, u32[]{:S(2)}) copy-start(s32[64,8]{0,1:T(8,128)} %param.17) | copy-start | bytes 6148
  28.2 1.6 copy-start.1
  31.1 20.1 %all-to-all-start.1 = ((bf16[32,64,128]{2,1,0:T(8,128)(2,1)}), bf16[32,64,128]{2,1,0:T(8,128)(2,1)S(1)}, u32[]{:S(2)}, u32[]{:S(2)}) async-start(bf16[32,64,128]{2,1,0:T(8,128)(2,1)} %shard_map.109), calls=%async_computation.1 | async-start | bytes 1048576 | tf_op jit(solution)/shard_map/all_to_all | solution.py:18
  51.4 73.5 %copy-start.4 = (bf16[128,4096]{1,0:T(8,128)(2,1)S(1)}, bf16[128,4096]{1,0:T(8,128)(2,1)}, u32[]{:S(2)}) copy-start(bf16[128,4096]{1,0:T(8,128)(2,1)} %w_ref.3) | copy-start | bytes 3145732
  87.1 42.0 %copy-start.9 = (f32[4096]{0:T(1024)S(1)}, f32[4096]{0:T(1024)}, u32[]{:S(2)}) copy-start(f32[4096]{0:T(1024)} %param.16) | copy-start | bytes 49156
  87.3 43.8 %copy-start.2 = (bf16[4096,128]{1,0:T(8,128)(2,1)S(1)}, bf16[4096,128]{1,0:T(8,128)(2,1)}, u32[]{:S(2)}) copy-start(bf16[4096,128]{1,0:T(8,128)(2,1)} %wg_ref.1) | copy-start | bytes 3145732
  87.3 43.8 %copy-start.3 = (bf16[4096,128]{1,0:T(8,128)(2,1)S(1)}, bf16[4096,128]{1,0:T(8,128)(2,1)}, u32[]{:S(2)}) copy-start(bf16[4096,128]{1,0:T(8,128)(2,1)} %wu_ref.1) | copy-start | bytes 3145732
  120.3 10.8 %collective-permute-start = (bf16[16,256,128]{2,1,0:T(8,128)(2,1)S(1)}, bf16[16,256,128]{2,1,0:T(8,128)(2,1)}, u32[]{:S(2)}, u32[]{:S(2)}) collective-permute-start(bf16[16,256,128]{2,1,0:T(8,128)(2,1)S(1)} %all_to_all.37.own_ref), channel_id=1, source_target_pairs={{0,1},{1,0},{2,3},{3,2},{4,5},{5,4},{6,7},{7,6},{8,9},{9,8},{10,11... | collective-permute-start | bytes 3145736 | tf_op jit(solution)/shard_map/ppermute | solution.py:22
  126.5 0.8 copy-start.5
  127.3 10.1 %collective-permute-start.2 = (bf16[4,128,512]{2,1,0:T(8,128)(2,1)}, bf16[4,128,512]{2,1,0:T(8,128)(2,1)}, u32[]{:S(2)}, u32[]{:S(2)}) collective-permute-start(bf16[4,128,512]{2,1,0:T(8,128)(2,1)} %get-tuple-element.8), channel_id=1, source_target_pairs={{0,1},{1,0},{2,3},{3,2},{4,5},{5,4},{6,7},{7,6},{8,9},{9,8},{10,11... | collective-permute-start | bytes 1572872 | tf_op jit(solution)/shard_map/ppermute | solution.py:22
  133.2 10.5 %copy-start.7 = (bf16[1,128,512]{2,1,0:T(8,128)(2,1)S(1)}, bf16[1,128,512]{2,1,0:T(8,128)(2,1)}, u32[]{:S(2)}) copy-start(bf16[1,128,512]{2,1,0:T(8,128)(2,1)} %get-tuple-element.10) | copy-start | bytes 393220
  133.2 15.7 %copy-start.6 = (bf16[1,128,512]{2,1,0:T(8,128)(2,1)S(1)}, bf16[1,128,512]{2,1,0:T(8,128)(2,1)}, u32[]{:S(2)}) copy-start(bf16[1,128,512]{2,1,0:T(8,128)(2,1)} %get-tuple-element.9) | copy-start | bytes 393220
  133.2 24.5 %copy-start.10 = (f32[64,8]{0,1:T(8,128)S(1)}, f32[64,8]{0,1:T(8,128)}, u32[]{:S(2)}) copy-start(f32[64,8]{0,1:T(8,128)} %param.18) | copy-start | bytes 6148
  133.9 20.2 %all-to-all-start.4 = ((bf16[4,256,128]{2,1,0:T(8,128)(2,1)}), bf16[4,256,128]{2,1,0:T(8,128)(2,1)S(1)}, u32[]{:S(2)}, u32[]{:S(2)}) async-start(bf16[4,256,128]{2,1,0:T(8,128)(2,1)} %broadcast_in_dim.22), calls=%async_computation.4 | async-start | bytes 524288 | tf_op jit(solution)/shard_map/all_to_all | solution.py:18
  139.4 18.4 %collective-permute-start.3 = (bf16[2,128,512]{2,1,0:T(8,128)(2,1)S(1)}, bf16[2,128,512]{2,1,0:T(8,128)(2,1)S(1)}, u32[]{:S(2)}, u32[]{:S(2)}) collective-permute-start(bf16[2,128,512]{2,1,0:T(8,128)(2,1)S(1)} %pad_maximum_fusion.1), channel_id=1, source_target_pairs={{0,2},{2,4},{4,6},{6,0},{1,3},{3,5},{5,7},{7,1},{8,10},{10,12},{12... | collective-permute-start | bytes 786440 | tf_op jit(solution)/shard_map/ppermute | solution.py:26
  143.7 23.4 %collective-permute-start.4 = (bf16[2,128,512]{2,1,0:T(8,128)(2,1)S(1)}, bf16[2,128,512]{2,1,0:T(8,128)(2,1)S(1)}, u32[]{:S(2)}, u32[]{:S(2)}) collective-permute-start(bf16[2,128,512]{2,1,0:T(8,128)(2,1)S(1)} %pad_maximum_fusion.2), channel_id=1, source_target_pairs={{0,4},{2,6},{4,0},{6,2},{1,5},{3,7},{5,1},{7,3},{8,12},{10,14},{12... | collective-permute-start | bytes 786440 | tf_op jit(solution)/shard_map/ppermute | solution.py:26
  148.9 19.9 %collective-permute-start.5 = (bf16[2,128,512]{2,1,0:T(8,128)(2,1)S(1)}, bf16[2,128,512]{2,1,0:T(8,128)(2,1)S(1)}, u32[]{:S(2)}, u32[]{:S(2)}) collective-permute-start(bf16[2,128,512]{2,1,0:T(8,128)(2,1)S(1)} %pad_maximum_fusion.3), channel_id=1, source_target_pairs={{0,6},{2,0},{4,2},{6,4},{1,7},{3,1},{5,3},{7,5},{8,14},{10,8},{12,... | collective-permute-start | bytes 786440 | tf_op jit(solution)/shard_map/ppermute | solution.py:26
  154.2 14.7 %collective-permute-start.1 = (bf16[4,256,128]{2,1,0:T(8,128)(2,1)S(1)}, bf16[4,256,128]{2,1,0:T(8,128)(2,1)S(1)}, u32[]{:S(2)}, u32[]{:S(2)}) collective-permute-start(bf16[4,256,128]{2,1,0:T(8,128)(2,1)S(1)} %all-to-all-done.4.own_ref), channel_id=1, source_target_pairs={{0,1},{1,0},{2,3},{3,2},{4,5},{5,4},{6,7},{7,6},{8,9},{9,8},{10,11... | collective-permute-start | bytes 786440 | tf_op jit(solution)/shard_map/ppermute | solution.py:22
  170.8 28.5 %all-to-all-start.5 = ((bf16[32,8,512]{2,1,0:T(8,128)(2,1)}), bf16[32,8,512]{2,1,0:T(8,128)(2,1)S(1)}, u32[]{:S(2)}, u32[]{:S(2)}) async-start(bf16[32,8,512]{2,1,0:T(8,128)(2,1)} %bitcast.9), calls=%async_computation.5 | async-start | bytes 524288 | tf_op jit(solution)/shard_map/all_to_all | solution.py:18
  200.2 19.7 %all-to-all-start.6 = ((bf16[32,2,512]{2,1,0:T(2,128)(2,1)}), bf16[32,2,512]{2,1,0:T(2,128)(2,1)S(1)}, u32[]{:S(2)}, u32[]{:S(2)}) async-start(bf16[32,2,512]{2,1,0:T(2,128)(2,1)} %reshape.54), calls=%async_computation.6 | async-start | bytes 131072 | tf_op jit(solution)/shard_map/all_to_all | solution.py:18
where the time goes:
time: 222 us; the launch traced here: 221 us
  blocking collectives  94.1 us (42%)
  waiting for transfers between devices  56.3 us (25%)
  starting transfers between devices  50.2 us (23%)
  local copies, waits for them, and re-layouts  7.2 us (3%)
  Pallas kernels  7 us (3%)
  other arithmetic  3.25 us (1%)
  matrix products  3.11 us (1%)
    all_to_all x3, blocking collectives, exchange(): return lax.all_to_all(value, axis, 0, 0, tiled=True)  94.1 us
    all_to_all x4, waiting for transfers between devices, exchange(): return lax.all_to_all(value, axis, 0, 0, tiled=True)  45.1 us
    all_to_all x4, starting transfers between devices, exchange(): return lax.all_to_all(value, axis, 0, 0, tiled=True)  25.6 us
    ppermute x3, starting transfers between devices, turn(): return lax.ppermute(value, 'yhi', [(i, (i + step) % NY) for i in range(NY)])  14.6 us
    ppermute x3, waiting for transfers between devices, turn(): return lax.ppermute(value, 'yhi', [(i, (i + step) % NY) for i in range(NY)])  11.1 us
    ppermute x3, starting transfers between devices, swap_cores(): return lax.ppermute(value, 'core', [(i, (i + 1) % NC) for i in range(NC)])  9.98 us
  transfers between devices with their start and end apart: 10, of which 5 were waited for; matrix products, arithmetic and copies ran while one was open for 3% of the time, Pallas kernels for 2%

commit v1 on v0

v1 whole, which is shorter than its diff:
```python
import math

import jax
import jax.numpy as jnp
from jax import lax
from jax.experimental import pallas as pl
from jax.experimental.pallas import tpu as pltpu
from jax.sharding import Mesh, PartitionSpec as P

CAP = 8
NX, NY, NC = 4, 4, 2
COL = ("x", "yhi", "core")
F32 = jnp.float32
BF16 = jnp.bfloat16


def exchange(value, axis):
    return lax.all_to_all(value, axis, 0, 0, tiled=True)


def swap_cores(value):
    return lax.ppermute(value, "core", [(i, (i + 1) % NC) for i in range(NC)])


def turn(value, step):
    return lax.ppermute(value, "yhi", [(i, (i + step) % NY) for i in range(NY)])


def to_all(value, axis, length):
    return exchange(jnp.broadcast_to(value[None], (length, *value.shape)), axis)


def attention(queries, keys, values):
    tok, heads, hd = queries.shape
    kv = keys.shape[1]
    grouped = queries.reshape(tok, kv, heads // kv, hd)
    scores = jnp.einsum(
        "tgqd,tgpd->tgqp", grouped, keys, preferred_element_type=F32
    ) / math.sqrt(hd)
    attn_weights = jax.nn.softmax(scores, axis=-1).astype(BF16)
    context = jnp.einsum("tgqp,tgpd->tgqd", attn_weights, values, preferred_element_type=F32)
    return context.astype(BF16).reshape(tok, heads * hd)


def hidden_units(rows_ref, gain_ref, wg0_ref, wg1_ref, wu0_ref, wu1_ref, act_ref):
    _, count, thin = rows_ref.shape
    hid = wg0_ref.shape[1]
    step = 2 * thin
    steps = gain_ref.shape[0]
    total = jnp.zeros((count, 4 * hid), F32)
    squares = jnp.zeros((count, step), F32)
    for at in range(steps):
        core, pair = divmod(at, steps // NC)
        first = 2 * pair * NC + core
        rows = jnp.concatenate([rows_ref[first], rows_ref[first + NC]], axis=1).astype(F32)
        squares = squares + rows * rows
        scaled = (rows * gain_ref[at : at + 1, :]).astype(BF16)
        here = slice(at * step, (at + 1) * step)
        weights = jnp.concatenate(
            [wg0_ref[here, :], wg1_ref[here, :], wu0_ref[here, :], wu1_ref[here, :]], axis=1
        )
        total = total + jnp.dot(scaled, weights, preferred_element_type=F32)
    inv = lax.rsqrt(jnp.sum(squares, axis=1, keepdims=True) / (steps * step) + 1e-06)
    gate = total[:, : 2 * hid] * inv
    up = total[:, 2 * hid :] * inv
    act_ref[...] = (gate / (1.0 + jnp.exp(-gate)) * up).astype(BF16)


def down_rows(own_ref, other_ref, wd0_ref, wd1_ref, wd2_ref, wd3_ref, out_ref):
    core, yhi = lax.axis_index("core"), lax.axis_index("yhi")
    half = own_ref.shape[1]
    for flip, ref in enumerate((own_ref, other_ref)):
        total = jnp.zeros((half, out_ref.shape[1]), F32)
        for step, wd_ref in enumerate((wd0_ref, wd1_ref, wd2_ref, wd3_ref)):
            act = ref[lax.rem(yhi + NY - step, NY)]
            weights = jnp.concatenate([wd_ref[flip], wd_ref[1 - flip]], axis=0)
            total = total + jnp.dot(act, weights, preferred_element_type=F32)
        at = pl.multiple_of(lax.rem(core + flip, NC) * half, half)
        out_ref[pl.ds(at, half), :] = total.astype(BF16)


def project(h_ref, w0_ref, w1_ref, out_ref):
    thin = out_ref.shape[2]
    for core, w_ref in enumerate((w0_ref, w1_ref)):
        both = jnp.dot(h_ref[...], w_ref[...], preferred_element_type=F32).astype(BF16)
        out_ref[core] = both[:, :thin]
        out_ref[NC + core] = both[:, thin:]


def projected(head_rows, out_proj, cols, thin):
    block, depth = head_rows.shape
    steps = cols // NC // 2
    return pl.pallas_call(
        project,
        grid=(steps,),
        out_shape=jax.ShapeDtypeStruct((cols, block, thin), BF16),
        in_specs=[
            pl.BlockSpec((block, depth), lambda g: (0, 0)),
            pl.BlockSpec((depth, 2 * thin), lambda g: (0, g)),
            pl.BlockSpec((depth, 2 * thin), lambda g: (0, g + steps)),
        ],
        out_specs=pl.BlockSpec((2 * NC, block, thin), lambda g: (g, 0, 0)),
    )(head_rows, out_proj, out_proj)


def cut_features(w_ref, same_ref, other_ref):
    core, yhi = lax.axis_index("core"), lax.axis_index("yhi")
    thin = same_ref.shape[2] // NX
    for flip, ref in enumerate((same_ref, other_ref)):
        c = lax.rem(core + flip, NC)
        for step in range(NY):
            y = lax.rem(yhi + step, NY)
            for x in range(NX):
                at = pl.multiple_of(((c * NX + x) * NY + y) * thin, thin)
                ref[step, :, x * thin : (x + 1) * thin] = w_ref[:, pl.ds(at, thin)]


def spread(in_ref, out_ref):
    rows, slots, thin = in_ref.shape
    per, half = slots // NX, rows // NC
    for x in range(NX):
        for core in range(NC):
            part = in_ref[core * half : (core + 1) * half, x * per : (x + 1) * per, :]
            part = part.reshape(half * per, thin)
            for y in range(NY):
                out_ref[(x * NY + y) * NC + core] = part


def join(in_ref, hidden_ref, out_ref):
    _, _, wide = in_ref.shape
    thin = wide // NX
    for y in range(NY):
        for core in range(NC):
            total = in_ref[y * NC + core].astype(F32)
            for x in range(1, NX):
                total = total + in_ref[(x * NY + y) * NC + core].astype(F32)
            for x in range(NX):
                at = ((core * NX + x) * NY + y) * thin
                here = slice(at, at + thin)
                done = total[:, x * thin : (x + 1) * thin] + hidden_ref[:, here].astype(F32)
                out_ref[:, here] = done.astype(BF16)


def local_call(body, outs, n_in):
    vmem = pl.BlockSpec(memory_space=pltpu.VMEM)
    out_shape = [jax.ShapeDtypeStruct(shape, BF16) for shape in outs]
    single = len(outs) == 1
    return pl.pallas_call(
        body,
        out_shape=out_shape[0] if single else out_shape,
        in_specs=[vmem] * n_in,
        out_specs=vmem if single else [vmem] * len(outs),
        compiler_params=pltpu.CompilerParams(vmem_limit_bytes=24 * 1024 * 1024),
    )


def shards(
    hidden, queries, keys, values, out_proj, norm_gain, routes, route_probs, w_gate, w_up, w_down
):
    rows = lax.axis_size("row")
    x, yhi, core = lax.axis_index("x"), lax.axis_index("yhi"), lax.axis_index("core")
    col_id = (x * NY + yhi) * NC + core
    tok_dev = queries.shape[0]
    block, d_model = hidden.shape
    cols = NX * NY * NC
    thin = d_model // cols
    wide = d_model // (NY * NC)
    count = rows * CAP

    route_weight = (route_probs / jnp.sum(route_probs, axis=-1, keepdims=True)).astype(BF16)
    earlier = (jnp.arange(block)[:, None] < jnp.arange(block)[None, :]).astype(BF16)
    slots = jnp.arange(CAP, dtype=F32)

    def slotted(experts):
        match = routes.T[None, :, :] == experts[:, None, None]
        hits = jnp.any(match, axis=1)
        before = jnp.dot(hits.astype(BF16), earlier, preferred_element_type=F32)
        place = hits[:, None, :] & (before[:, None, :] == slots[None, :, None])
        return match, place.astype(BF16)

    _, place = slotted(jnp.arange(rows * NX, dtype=jnp.int32))
    place = place.reshape(rows * NX * CAP, block)
    match, mine = slotted(jnp.arange(rows, dtype=jnp.int32) * NX + x)
    chosen = jnp.sum(jnp.where(match, route_weight.T[None], jnp.zeros((), BF16)), axis=1)
    combine = (mine * chosen[:, None, :]).reshape(count, block).T

    gate_other, up_other = swap_cores(w_gate), swap_cores(w_up)

    context = attention(queries, keys, values)
    heads_out = jnp.moveaxis(context.reshape(tok_dev, cols, -1), 1, 0)
    head_rows = exchange(heads_out, COL).reshape(block, -1)

    part = projected(head_rows, out_proj, cols, thin)
    attn = jnp.sum(exchange(part, COL).astype(F32), axis=0)
    own_at = ((core * NX + x) * NY + yhi) * thin
    resid = lax.dynamic_slice_in_dim(hidden, own_at, thin, 1).astype(F32) + attn

    outgoing = jnp.dot(place, resid.astype(BF16), preferred_element_type=F32).astype(BF16)
    arrived = exchange(outgoing.reshape(rows, NX * CAP, thin), "row")

    hid = w_down.shape[0]
    same, rest = local_call(cut_features, [(NY, hid, wide)] * 2, 1)(w_down)
    pieces = [jnp.stack(pair) for pair in zip(same, swap_cores(rest))]
    down = [pieces[0]] + [turn(pieces[step], step) for step in (1, 3, 2)]
    down = [down[0], down[1], down[3], down[2]]

    by_expert = local_call(spread, [(cols, count // NC, thin)], 1)(arrived)
    features = exchange(by_expert, COL)
    act = local_call(hidden_units, [(count // NC, NC * hid)], 6)(
        features, norm_gain.reshape(-1, 2 * thin), w_gate, gate_other, w_up, up_other
    )
    own_act = to_all(act, "yhi", NY)
    other_act = swap_cores(own_act)
    back = local_call(down_rows, [(count, wide)], 6)(own_act, other_act, *down)
    returned = exchange(back.reshape(rows, CAP, wide), "row").reshape(count, wide)

    own_hidden = lax.dynamic_slice_in_dim(hidden, col_id * tok_dev, tok_dev, 0)
    own_hidden, returned = lax.optimization_barrier((own_hidden, returned))

    attn_here = jnp.concatenate([jnp.where(x == i, attn, 0.0) for i in range(NX)], axis=1)
    mixed = jnp.dot(combine, returned, preferred_element_type=F32) + attn_here
    final = exchange(mixed.astype(BF16).reshape(cols, tok_dev, wide), COL)
    return local_call(join, [(tok_dev, d_model)], 2)(final, own_hidden)


def solution(mesh):
    rows = mesh.shape["row"]
    fine = Mesh(mesh.devices.reshape(rows, NX, NY, NC), ("row",) + COL)
    every = ("row",) + COL
    return jax.shard_map(
        shards,
        mesh=fine,
        in_specs=(
            P("row", None),
            P(every, None, None),
            P(every, None, None, None),
            P(every, None, None, None),
            P(COL, None),
            P(),
            P("row", None),
            P("row", None),
            P(None, every),
            P(None, every),
            P(every, None),
        ),
        out_specs=P(every, None),
        check_vma=False,
    )
```

time: 222 us -> 217 us (0.977)
  blocking collectives: 94.1 us -> 81.5 us
  waiting for transfers between devices: 56.3 us -> 65.6 us
  Pallas kernels: 7 us -> 12.2 us
  starting transfers between devices: 50.2 us -> 46.4 us
  other arithmetic: 3.25 us -> 0.84 us
    all_to_all x3, blocking collectives: 94.1 us -> 81.5 us  [exchange(): return lax.all_to_all(value, axis, 0, 0, tiled=True)]
    all_to_all x4, waiting for transfers between devices: 45.1 us -> 53.8 us  [exchange(): return lax.all_to_all(value, axis, 0, 0, tiled=True)]
    pallas_call x5 -> x6, Pallas kernels: 7 us -> 12.2 us  [the longest x1 5.98 us: projected(): pl.pallas_call(project, grid=(steps,), out_shape=jax.ShapeDtypeStruct((co...]
    all_to_all x4, starting transfers between devices: 25.6 us -> 20.9 us  [exchange(): return lax.all_to_all(value, axis, 0, 0, tiled=True)]
    ppermute x3 -> x4, starting transfers between devices: 9.98 us -> 10.9 us  [swap_cores(): return lax.ppermute(value, 'core', [(i, (i + 1) % NC) for i in range(NC)])]
  transfers between devices with their start and end apart: 10 -> 11, of which waited for: 5 -> 6; matrix products, arithmetic and copies ran while one was open for 3% -> 2% of each run, Pallas kernels for 2% -> 2%
where the time goes in v1:
time: 217 us; the launch traced here: 216 us
  blocking collectives  81.5 us (38%)
  waiting for transfers between devices  65.6 us (30%)
  starting transfers between devices  46.4 us (21%)
  Pallas kernels  12.2 us (6%)
  local copies, waits for them, and re-layouts  5.82 us (3%)
  matrix products  3.21 us (1%)
    all_to_all x3, blocking collectives, exchange(): return lax.all_to_all(value, axis, 0, 0, tiled=True)  81.5 us
    all_to_all x4, waiting for transfers between devices, exchange(): return lax.all_to_all(value, axis, 0, 0, tiled=True)  53.8 us
    all_to_all x4, starting transfers between devices, exchange(): return lax.all_to_all(value, axis, 0, 0, tiled=True)  20.9 us
    ppermute x3, starting transfers between devices, turn(): return lax.ppermute(value, 'yhi', [(i, (i + step) % NY) for i in range(NY)])  14.6 us
    ppermute x3, waiting for transfers between devices, turn(): return lax.ppermute(value, 'yhi', [(i, (i + step) % NY) for i in range(NY)])  11.8 us
    ppermute x4, starting transfers between devices, swap_cores(): return lax.ppermute(value, 'core', [(i, (i + 1) % NC) for i in range(NC)])  10.9 us
    pallas_call x1, Pallas kernels, projected(): pl.pallas_call(project, grid=(steps,), out_shape=jax.ShapeDtypeStruct((co...  5.98 us
  transfers between devices with their start and end apart: 11, of which 6 were waited for; matrix products, arithmetic and copies ran while one was open for 2% of the time, Pallas kernels for 2%

profile of v1, /device:TPU:1, one launch (start us, length us, event | category | flops | bytes accessed | tf_op | source)
XLA Modules:
  0.0 216.0 jit_solution(13876283745564181794)
XLA Ops:
  0.0 1.1 convolution_multiply_fusion
  1.1 0.2 fusion.31
  1.3 0.3 convolution_convert_fusion.1
  1.7 26.5 %all_to_all.35 = bf16[32,2,256]{2,1,0:T(2,128)(2,1)S(1)} all-to-all(bf16[32,2,256]{2,1,0:T(2,128)(2,1)S(1)} %bitcast.47), channel_id=1, replica_groups=mesh['row'=32,'x'=4,'yhi'=4,'core'=2] {'x','yhi','core'}, dimensions={0} | all-to-all | bytes 65536 | tf_op jit(solution)/shard_map/all_to_all | solution.py:18
  28.2 0.6 reshape.47.h_ref
  28.8 6.0 %shard_map.109 = bf16[32,64,128]{2,1,0:T(8,128)(2,1)} custom-call(bf16[64,256]{1,0:T(8,128)(2,1)} %reshape.47.h_ref, bf16[256,4096]{1,0:T(8,128)(2,1)} %w1_ref.1, bf16[256,4096]{1,0:T(8,128)(2,1)} %w1_ref.1), custom_call_target="tpu_custom_call" | custom-call | tf_op jit(solution)/shard_map/pallas_call | solution.py:93
  34.8 3.9 %all-to-all-start.1 = ((bf16[32,64,128]{2,1,0:T(8,128)(2,1)}), bf16[32,64,128]{2,1,0:T(8,128)(2,1)S(1)}, u32[]{:S(2)}, u32[]{:S(2)}) async-start(bf16[32,64,128]{2,1,0:T(8,128)(2,1)} %shard_map.109), calls=%async_computation.1 | async-start | bytes 1048576 | tf_op jit(solution)/shard_map/all_to_all | solution.py:18
  38.8 0.1 fusion.9
  38.9 0.1 copy.16
  39.1 0.1 eq.93
  39.2 0.2 fusion.22
  39.4 15.6 %all-to-all-done.1 = bf16[32,64,128]{2,1,0:T(8,128)(2,1)S(1)} async-done(((bf16[32,64,128]{2,1,0:T(8,128)(2,1)}), bf16[32,64,128]{2,1,0:T(8,128)(2,1)S(1)}, u32[]{:S(2)}, u32[]{:S(2)}) %all-to-all-start.1) | async-done | bytes 524320 | tf_op jit(solution)/shard_map/all_to_all | solution.py:18
  55.0 0.1 convert_reduce_fusion
  55.0 0.0 copy-start.2
  55.1 0.0 copy-start.1
  55.1 1.2 convolution_convert_fusion
  56.3 34.6 %all_to_all.36.in_ref = bf16[32,32,128]{2,1,0:T(8,128)(2,1)S(1)} all-to-all(bf16[32,32,128]{2,1,0:T(8,128)(2,1)S(1)} %bitcast.45), channel_id=1, replica_groups=mesh['row'=32,'x'=4,'yhi'=4,'core'=2] {'row'}, dimensions={0} | all-to-all | bytes 524288 | tf_op jit(solution)/shard_map/all_to_all | solution.py:18
  90.9 1.1 shard_map.110
  92.0 7.9 %all-to-all-start.3 = ((bf16[32,128,128]{2,1,0:T(8,128)(2,1)}), bf16[32,128,128]{2,1,0:T(8,128)(2,1)S(1)}, u32[]{:S(2)}, u32[]{:S(2)}) async-start(bf16[32,128,128]{2,1,0:T(8,128)(2,1)} %shard_map.110), calls=%async_computation.3 | async-start | bytes 2097152 | tf_op jit(solution)/shard_map/all_to_all | solution.py:18
  99.9 2.1 collective-permute-start
  102.1 2.2 %collective-permute-start.1 = (bf16[4096,128]{1,0:T(8,128)(2,1)}, bf16[4096,128]{1,0:T(8,128)(2,1)}, u32[]{:S(2)}, u32[]{:S(2)}) collective-permute-start(bf16[4096,128]{1,0:T(8,128)(2,1)} %wu0_ref.1), channel_id=1, source_target_pairs={{0,1},{1,0},{2,3},{3,2},{4,5},{5,4},{6,7},{7,6},{8,9},{9,8},{10,11... | collective-permute-start | bytes 3145736 | tf_op jit(solution)/shard_map/ppermute | solution.py:22
  104.3 1.1 shard_map.112
  105.4 0.8 copy-done.4
  106.1 2.1 collective-permute-start.3
  108.3 1.1 fusion.29
  109.5 19.2 %all-to-all-done.3.rows_ref = bf16[32,128,128]{2,1,0:T(8,128)(2,1)S(1)} async-done(((bf16[32,128,128]{2,1,0:T(8,128)(2,1)}), bf16[32,128,128]{2,1,0:T(8,128)(2,1)S(1)}, u32[]{:S(2)}, u32[]{:S(2)}) %all-to-all-start.3) | async-done | bytes 1048608 | tf_op jit(solution)/shard_map/all_to_all | solution.py:18
  128.7 1.2 copy-done.3
  130.0 2.3 %shard_map.111 = bf16[128,256]{1,0:T(8,128)(2,1)S(1)} custom-call(bf16[32,128,128]{2,1,0:T(8,128)(2,1)S(1)} %all-to-all-done.3.rows_ref, f32[16,256]{1,0:T(8,128)S(1)} %reshape.49.gain_ref, bf16[4096,128]{1,0:T(8,128)(2,1)S(1)} %copy-done.2, bf16[4096,128]{1,0:T(8,128)(2,1)} %collective-permute-done.wg1_ref, bf16[4096,128]{1,0:T(8,128)(2,1)S(1)} %copy-done.3, ...), custom_call_target="tpu_custom_call" | custom-call | tf_op jit(solution)/shard_map/pallas_call | solution.py:209
  132.2 0.7 broadcast_in_dim.22
  133.0 3.4 %all-to-all-start.4 = ((bf16[4,128,256]{2,1,0:T(8,128)(2,1)}), bf16[4,128,256]{2,1,0:T(8,128)(2,1)S(1)}, u32[]{:S(2)}, u32[]{:S(2)}) async-start(bf16[4,128,256]{2,1,0:T(8,128)(2,1)} %broadcast_in_dim.22), calls=%async_computation.4 | async-start | bytes 524288 | tf_op jit(solution)/shard_map/all_to_all | solution.py:18
  136.5 4.2 %collective-permute-start.4 = (bf16[2,128,512]{2,1,0:T(8,128)(2,1)S(1)}, bf16[2,128,512]{2,1,0:T(8,128)(2,1)S(1)}, u32[]{:S(2)}, u32[]{:S(2)}) collective-permute-start(bf16[2,128,512]{2,1,0:T(8,128)(2,1)S(1)} %pad_maximum_fusion.1), channel_id=1, source_target_pairs={{0,2},{2,4},{4,6},{6,0},{1,3},{3,5},{5,7},{7,1},{8,10},{10,12},{12... | collective-permute-start | bytes 786440 | tf_op jit(solution)/shard_map/ppermute | solution.py:26
  140.7 5.2 %collective-permute-start.5 = (bf16[2,128,512]{2,1,0:T(8,128)(2,1)S(1)}, bf16[2,128,512]{2,1,0:T(8,128)(2,1)S(1)}, u32[]{:S(2)}, u32[]{:S(2)}) collective-permute-start(bf16[2,128,512]{2,1,0:T(8,128)(2,1)S(1)} %pad_maximum_fusion.2), channel_id=1, source_target_pairs={{0,4},{2,6},{4,0},{6,2},{1,5},{3,7},{5,1},{7,3},{8,12},{10,14},{12... | collective-permute-start | bytes 786440 | tf_op jit(solution)/shard_map/ppermute | solution.py:26
  146.0 5.2 %collective-permute-start.6 = (bf16[2,128,512]{2,1,0:T(8,128)(2,1)S(1)}, bf16[2,128,512]{2,1,0:T(8,128)(2,1)S(1)}, u32[]{:S(2)}, u32[]{:S(2)}) collective-permute-start(bf16[2,128,512]{2,1,0:T(8,128)(2,1)S(1)} %pad_maximum_fusion.3), channel_id=1, source_target_pairs={{0,6},{2,0},{4,2},{6,4},{1,7},{3,1},{5,3},{7,5},{8,14},{10,8},{12,... | collective-permute-start | bytes 786440 | tf_op jit(solution)/shard_map/ppermute | solution.py:26
  151.2 4.4 %collective-permute-start.2 = (bf16[4,128,256]{2,1,0:T(8,128)(2,1)S(1)}, bf16[4,128,256]{2,1,0:T(8,128)(2,1)S(1)}, u32[]{:S(2)}, u32[]{:S(2)}) collective-permute-start(bf16[4,128,256]{2,1,0:T(8,128)(2,1)S(1)} %all-to-all-done.4.own_ref), channel_id=1, source_target_pairs={{0,1},{1,0},{2,3},{3,2},{4,5},{5,4},{6,7},{7,6},{8,9},{9,8},{10,11... | collective-permute-start | bytes 786440 | tf_op jit(solution)/shard_map/ppermute | solution.py:22
  155.7 0.1 eq.84
  155.8 0.1 fusion.14
  155.9 0.8 collective-permute-done.4.wd1_ref
  156.8 5.9 %collective-permute-done.5.wd2_ref = bf16[2,128,512]{2,1,0:T(8,128)(2,1)S(1)} collective-permute-done((bf16[2,128,512]{2,1,0:T(8,128)(2,1)S(1)}, bf16[2,128,512]{2,1,0:T(8,128)(2,1)S(1)}, u32[]{:S(2)}, u32[]{:S(2)}) %collective-permute-start.5) | collective-permute-done | bytes 262176 | tf_op jit(solution)/shard_map/ppermute | solution.py:26
  162.7 5.0 %collective-permute-done.6.wd3_ref = bf16[2,128,512]{2,1,0:T(8,128)(2,1)S(1)} collective-permute-done((bf16[2,128,512]{2,1,0:T(8,128)(2,1)S(1)}, bf16[2,128,512]{2,1,0:T(8,128)(2,1)S(1)}, u32[]{:S(2)}, u32[]{:S(2)}) %collective-permute-start.6) | collective-permute-done | bytes 262176 | tf_op jit(solution)/shard_map/ppermute | solution.py:26
  167.7 1.1 shard_map.113
  168.8 5.6 %all-to-all-start.5 = ((bf16[32,8,512]{2,1,0:T(8,128)(2,1)}), bf16[32,8,512]{2,1,0:T(8,128)(2,1)S(1)}, u32[]{:S(2)}, u32[]{:S(2)}) async-start(bf16[32,8,512]{2,1,0:T(8,128)(2,1)} %bitcast.10), calls=%async_computation.5 | async-start | bytes 524288 | tf_op jit(solution)/shard_map/all_to_all | solution.py:18
  174.5 0.1 compare_reduce_fusion
  174.6 0.1 fusion.23
  174.7 0.9 constant_dynamic-slice_fusion.hidden_ref
  175.6 19.0 %all-to-all-done.5 = bf16[32,8,512]{2,1,0:T(8,128)(2,1)S(1)} async-done(((bf16[32,8,512]{2,1,0:T(8,128)(2,1)}), bf16[32,8,512]{2,1,0:T(8,128)(2,1)S(1)}, u32[]{:S(2)}, u32[]{:S(2)}) %all-to-all-start.5) | async-done | bytes 262176 | tf_op jit(solution)/shard_map/all_to_all | solution.py:18
  194.6 0.3 fusion.1
  195.0 20.4 %all_to_all.37.in_ref = bf16[32,2,512]{2,1,0:T(2,128)(2,1)S(1)} all-to-all(bf16[32,2,512]{2,1,0:T(2,128)(2,1)S(1)} %reshape.52), channel_id=1, replica_groups=mesh['row'=32,'x'=4,'yhi'=4,'core'=2] {'x','yhi','core'}, dimensions={0} | all-to-all | bytes 131072 | tf_op jit(solution)/shard_map/all_to_all | solution.py:18
  215.4 0.6 shard_map.114
  (32 shorter events, 0.4 us)
Async XLA Ops:
  0.0 1.3 copy-start
  28.8 9.9 %copy-start.5 = (s32[64,8]{0,1:T(8,128)S(1)}, s32[64,8]{0,1:T(8,128)}, u32[]{:S(2)}) copy-start(s32[64,8]{0,1:T(8,128)} %param.17) | copy-start | bytes 6148
  34.8 20.1 %all-to-all-start.1 = ((bf16[32,64,128]{2,1,0:T(8,128)(2,1)}), bf16[32,64,128]{2,1,0:T(8,128)(2,1)S(1)}, u32[]{:S(2)}, u32[]{:S(2)}) async-start(bf16[32,64,128]{2,1,0:T(8,128)(2,1)} %shard_map.109), calls=%async_computation.1 | async-start | bytes 1048576 | tf_op jit(solution)/shard_map/all_to_all | solution.py:18
  55.0 44.9 %copy-start.2 = (bf16[4096,128]{1,0:T(8,128)(2,1)S(1)}, bf16[4096,128]{1,0:T(8,128)(2,1)}, u32[]{:S(2)}) copy-start(bf16[4096,128]{1,0:T(8,128)(2,1)} %wg0_ref.1) | copy-start | bytes 3145732
  55.1 49.2 %copy-start.1 = (bf16[128,4096]{1,0:T(8,128)(2,1)S(1)}, bf16[128,4096]{1,0:T(8,128)(2,1)}, u32[]{:S(2)}) copy-start(bf16[128,4096]{1,0:T(8,128)(2,1)} %w_ref.1) | copy-start | bytes 3145732
  90.9 17.4 %copy-start.6 = (f32[4096]{0:T(1024)S(1)}, f32[4096]{0:T(1024)}, u32[]{:S(2)}) copy-start(f32[4096]{0:T(1024)} %param.16) | copy-start | bytes 49156
  90.9 17.4 %copy-start.7 = (f32[64,8]{0,1:T(8,128)S(1)}, f32[64,8]{0,1:T(8,128)}, u32[]{:S(2)}) copy-start(f32[64,8]{0,1:T(8,128)} %param.18) | copy-start | bytes 6148
  92.0 36.7 %all-to-all-start.3 = ((bf16[32,128,128]{2,1,0:T(8,128)(2,1)}), bf16[32,128,128]{2,1,0:T(8,128)(2,1)S(1)}, u32[]{:S(2)}, u32[]{:S(2)}) async-start(bf16[32,128,128]{2,1,0:T(8,128)(2,1)} %shard_map.110), calls=%async_computation.3 | async-start | bytes 2097152 | tf_op jit(solution)/shard_map/all_to_all | solution.py:18
  99.9 9.6 %collective-permute-start = (bf16[4096,128]{1,0:T(8,128)(2,1)S(1)}, bf16[4096,128]{1,0:T(8,128)(2,1)}, u32[]{:S(2)}, u32[]{:S(2)}) collective-permute-start(bf16[4096,128]{1,0:T(8,128)(2,1)S(1)} %copy-done.2), channel_id=1, source_target_pairs={{0,1},{1,0},{2,3},{3,2},{4,5},{5,4},{6,7},{7,6},{8,9},{9,8},{10,11... | collective-permute-start | bytes 3145736 | tf_op jit(solution)/shard_map/ppermute | solution.py:22
  102.1 7.4 %collective-permute-start.1 = (bf16[4096,128]{1,0:T(8,128)(2,1)}, bf16[4096,128]{1,0:T(8,128)(2,1)}, u32[]{:S(2)}, u32[]{:S(2)}) collective-permute-start(bf16[4096,128]{1,0:T(8,128)(2,1)} %wu0_ref.1), channel_id=1, source_target_pairs={{0,1},{1,0},{2,3},{3,2},{4,5},{5,4},{6,7},{7,6},{8,9},{9,8},{10,11... | collective-permute-start | bytes 3145736 | tf_op jit(solution)/shard_map/ppermute | solution.py:22
  105.4 0.8 copy-start.4
  106.1 30.2 %collective-permute-start.3 = (bf16[4,128,512]{2,1,0:T(8,128)(2,1)}, bf16[4,128,512]{2,1,0:T(8,128)(2,1)S(1)}, u32[]{:S(2)}, u32[]{:S(2)}) collective-permute-start(bf16[4,128,512]{2,1,0:T(8,128)(2,1)} %get-tuple-element.10), channel_id=1, source_target_pairs={{0,1},{1,0},{2,3},{3,2},{4,5},{5,4},{6,7},{7,6},{8,9},{9,8},{10,11... | collective-permute-start | bytes 1572872 | tf_op jit(solution)/shard_map/ppermute | solution.py:22
  128.7 1.2 copy-start.3
  133.0 18.2 %all-to-all-start.4 = ((bf16[4,128,256]{2,1,0:T(8,128)(2,1)}), bf16[4,128,256]{2,1,0:T(8,128)(2,1)S(1)}, u32[]{:S(2)}, u32[]{:S(2)}) async-start(bf16[4,128,256]{2,1,0:T(8,128)(2,1)} %broadcast_in_dim.22), calls=%async_computation.4 | async-start | bytes 524288 | tf_op jit(solution)/shard_map/all_to_all | solution.py:18
  136.5 20.3 %collective-permute-start.4 = (bf16[2,128,512]{2,1,0:T(8,128)(2,1)S(1)}, bf16[2,128,512]{2,1,0:T(8,128)(2,1)S(1)}, u32[]{:S(2)}, u32[]{:S(2)}) collective-permute-start(bf16[2,128,512]{2,1,0:T(8,128)(2,1)S(1)} %pad_maximum_fusion.1), channel_id=1, source_target_pairs={{0,2},{2,4},{4,6},{6,0},{1,3},{3,5},{5,7},{7,1},{8,10},{10,12},{12... | collective-permute-start | bytes 786440 | tf_op jit(solution)/shard_map/ppermute | solution.py:26
  140.7 22.0 %collective-permute-start.5 = (bf16[2,128,512]{2,1,0:T(8,128)(2,1)S(1)}, bf16[2,128,512]{2,1,0:T(8,128)(2,1)S(1)}, u32[]{:S(2)}, u32[]{:S(2)}) collective-permute-start(bf16[2,128,512]{2,1,0:T(8,128)(2,1)S(1)} %pad_maximum_fusion.2), channel_id=1, source_target_pairs={{0,4},{2,6},{4,0},{6,2},{1,5},{3,7},{5,1},{7,3},{8,12},{10,14},{12... | collective-permute-start | bytes 786440 | tf_op jit(solution)/shard_map/ppermute | solution.py:26
  146.0 21.7 %collective-permute-start.6 = (bf16[2,128,512]{2,1,0:T(8,128)(2,1)S(1)}, bf16[2,128,512]{2,1,0:T(8,128)(2,1)S(1)}, u32[]{:S(2)}, u32[]{:S(2)}) collective-permute-start(bf16[2,128,512]{2,1,0:T(8,128)(2,1)S(1)} %pad_maximum_fusion.3), channel_id=1, source_target_pairs={{0,6},{2,0},{4,2},{6,4},{1,7},{3,1},{5,3},{7,5},{8,14},{10,8},{12,... | collective-permute-start | bytes 786440 | tf_op jit(solution)/shard_map/ppermute | solution.py:26
  151.2 16.5 %collective-permute-start.2 = (bf16[4,128,256]{2,1,0:T(8,128)(2,1)S(1)}, bf16[4,128,256]{2,1,0:T(8,128)(2,1)S(1)}, u32[]{:S(2)}, u32[]{:S(2)}) collective-permute-start(bf16[4,128,256]{2,1,0:T(8,128)(2,1)S(1)} %all-to-all-done.4.own_ref), channel_id=1, source_target_pairs={{0,1},{1,0},{2,3},{3,2},{4,5},{5,4},{6,7},{7,6},{8,9},{9,8},{10,11... | collective-permute-start | bytes 786440 | tf_op jit(solution)/shard_map/ppermute | solution.py:22
  168.8 25.8 %all-to-all-start.5 = ((bf16[32,8,512]{2,1,0:T(8,128)(2,1)}), bf16[32,8,512]{2,1,0:T(8,128)(2,1)S(1)}, u32[]{:S(2)}, u32[]{:S(2)}) async-start(bf16[32,8,512]{2,1,0:T(8,128)(2,1)} %bitcast.10), calls=%async_computation.5 | async-start | bytes 524288 | tf_op jit(solution)/shard_map/all_to_all | solution.py:18

commit v2 on v1

--- a/solution.py
+++ b/solution.py
@@ -79,28 +79,44 @@
         out_ref[pl.ds(at, half), :] = total.astype(BF16)
 
 
-def project(h_ref, w0_ref, w1_ref, out_ref):
+CHUNKS = 4
+
+
+def project(h_ref, w_ref, out_ref, held, sems):
     thin = out_ref.shape[2]
-    for core, w_ref in enumerate((w0_ref, w1_ref)):
-        both = jnp.dot(h_ref[...], w_ref[...], preferred_element_type=F32).astype(BF16)
-        out_ref[core] = both[:, :thin]
-        out_ref[NC + core] = both[:, thin:]
+    chunk = held.shape[2]
+    half = out_ref.shape[0] // NC
+    copies = [
+        pltpu.make_async_copy(w_ref.at[:, pl.ds(i * chunk, chunk)], held.at[i], sems.at[i])
+        for i in range(CHUNKS)
+    ]
+    for copy in copies:
+        copy.start()
+    rows = h_ref[...]
+    for i, copy in enumerate(copies):
+        copy.wait()
+        for at in range(0, chunk, 2 * thin):
+            both = jnp.dot(
+                rows, held[i, :, at : at + 2 * thin], preferred_element_type=F32
+            ).astype(BF16)
+            core, p = divmod((i * chunk + at) // thin, half)
+            out_ref[p * NC + core] = both[:, :thin]
+            out_ref[(p + 1) * NC + core] = both[:, thin:]
 
 
 def projected(head_rows, out_proj, cols, thin):
     block, depth = head_rows.shape
-    steps = cols // NC // 2
+    vmem = pl.BlockSpec(memory_space=pltpu.VMEM)
     return pl.pallas_call(
         project,
-        grid=(steps,),
         out_shape=jax.ShapeDtypeStruct((cols, block, thin), BF16),
-        in_specs=[
-            pl.BlockSpec((block, depth), lambda g: (0, 0)),
-            pl.BlockSpec((depth, 2 * thin), lambda g: (0, g)),
-            pl.BlockSpec((depth, 2 * thin), lambda g: (0, g + steps)),
+        in_specs=[vmem, pl.BlockSpec(memory_space=pl.ANY)],
+        out_specs=vmem,
+        scratch_shapes=[
+            pltpu.VMEM((CHUNKS, depth, cols * thin // CHUNKS), BF16),
+            pltpu.SemaphoreType.DMA((CHUNKS,)),
         ],
-        out_specs=pl.BlockSpec((2 * NC, block, thin), lambda g: (g, 0, 0)),
-    )(head_rows, out_proj, out_proj)
+    )(head_rows, out_proj)
 
 
 def cut_features(w_ref, same_ref, other_ref):
@@ -191,16 +207,21 @@
     head_rows = exchange(heads_out, COL).reshape(block, -1)
 
     part = projected(head_rows, out_proj, cols, thin)
-    attn = jnp.sum(exchange(part, COL).astype(F32), axis=0)
+    part = exchange(part, COL)
+    attn = jnp.sum(part.astype(F32), axis=0)
     own_at = ((core * NX + x) * NY + yhi) * thin
-    resid = lax.dynamic_slice_in_dim(hidden, own_at, thin, 1).astype(F32) + attn
+    place, hidden_part = lax.optimization_barrier(
+        (place, lax.dynamic_slice_in_dim(hidden, own_at, thin, 1))
+    )
+    resid = hidden_part.astype(F32) + attn
 
     outgoing = jnp.dot(place, resid.astype(BF16), preferred_element_type=F32).astype(BF16)
     arrived = exchange(outgoing.reshape(rows, NX * CAP, thin), "row")
 
     hid = w_down.shape[0]
     same, rest = local_call(cut_features, [(NY, hid, wide)] * 2, 1)(w_down)
-    pieces = [jnp.stack(pair) for pair in zip(same, swap_cores(rest))]
+    rest = swap_cores(rest)
+    pieces = [jnp.stack(pair) for pair in zip(same, rest)]
     down = [pieces[0]] + [turn(pieces[step], step) for step in (1, 3, 2)]
     down = [down[0], down[1], down[3], down[2]]
 

time: 217 us -> 216 us (level)
  Pallas kernels: 12.2 us -> 9.7 us
  waiting for transfers between devices: 65.6 us -> 67.9 us
    pallas_call x1, Pallas kernels: 5.98 us -> 3.47 us  [projected(): pl.pallas_call(project, out_shape=jax.ShapeDtypeStruct((cols, block, thin...]
    all_to_all x4, waiting for transfers between devices: 53.8 us -> 56.3 us  [exchange(): return lax.all_to_all(value, axis, 0, 0, tiled=True)]
  transfers between devices with their start and end apart: 11 -> 11, of which waited for: 6 -> 6; matrix products, arithmetic and copies ran while one was open for 2% -> 1% of each run, Pallas kernels for 2% -> 2%
where the time goes in v2:
time: 216 us; the launch traced here: 215 us
  blocking collectives  81.7 us (38%)
  waiting for transfers between devices  67.9 us (31%)
  starting transfers between devices  46.6 us (22%)
  Pallas kernels  9.7 us (4%)
  local copies, waits for them, and re-layouts  4.35 us (2%)
  matrix products  3.16 us (1%)
    all_to_all x3, blocking collectives, exchange(): return lax.all_to_all(value, axis, 0, 0, tiled=True)  81.7 us
    all_to_all x4, waiting for transfers between devices, exchange(): return lax.all_to_all(value, axis, 0, 0, tiled=True)  56.3 us
    all_to_all x4, starting transfers between devices, exchange(): return lax.all_to_all(value, axis, 0, 0, tiled=True)  21 us
    ppermute x3, starting transfers between devices, turn(): return lax.ppermute(value, 'yhi', [(i, (i + step) % NY) for i in range(NY)])  14.6 us
    ppermute x3, waiting for transfers between devices, turn(): return lax.ppermute(value, 'yhi', [(i, (i + step) % NY) for i in range(NY)])  11.6 us
    ppermute x4, starting transfers between devices, swap_cores(): return lax.ppermute(value, 'core', [(i, (i + 1) % NC) for i in range(NC)])  10.9 us
  transfers between devices with their start and end apart: 11, of which 6 were waited for; matrix products, arithmetic and copies ran while one was open for 1% of the time, Pallas kernels for 2%

profile of v2, /device:TPU:1, one launch (start us, length us, event | category | flops | bytes accessed | tf_op | source)
XLA Modules:
  0.0 214.8 jit_solution(13589857337152177484)
XLA Ops:
  0.0 1.1 convolution_multiply_fusion
  1.1 0.2 fusion.25
  1.4 0.0 copy-start.4
  1.4 1.2 convolution_convert_fusion.1
  2.6 26.5 %all_to_all.35 = bf16[32,2,256]{2,1,0:T(2,128)(2,1)S(1)} all-to-all(bf16[32,2,256]{2,1,0:T(2,128)(2,1)S(1)} %bitcast.46), channel_id=1, replica_groups=mesh['row'=32,'x'=4,'yhi'=4,'core'=2] {'x','yhi','core'}, dimensions={0} | all-to-all | bytes 65536 | tf_op jit(solution)/shard_map/all_to_all | solution.py:18
  29.2 0.6 reshape.47.h_ref
  29.8 3.5 %shard_map.109 = bf16[32,64,128]{2,1,0:T(8,128)(2,1)} custom-call(bf16[64,256]{1,0:T(8,128)(2,1)} %reshape.47.h_ref, bf16[256,4096]{1,0:T(8,128)(2,1)} %w_ref.2), custom_call_target="tpu_custom_call" | custom-call | tf_op jit(solution)/shard_map/pallas_call | solution.py:110
  33.3 3.9 %all-to-all-start.1 = ((bf16[32,64,128]{2,1,0:T(8,128)(2,1)}), bf16[32,64,128]{2,1,0:T(8,128)(2,1)S(1)}, u32[]{:S(2)}, u32[]{:S(2)}) async-start(bf16[32,64,128]{2,1,0:T(8,128)(2,1)} %shard_map.109), calls=%async_computation.1 | async-start | bytes 1048576 | tf_op jit(solution)/shard_map/all_to_all | solution.py:18
  37.2 0.1 fusion.6
  37.4 0.1 copy.16
  37.5 0.1 eq.93
  37.6 0.2 fusion.18
  37.9 0.2 fusion.5
  38.1 15.3 %all-to-all-done.1 = bf16[32,64,128]{2,1,0:T(8,128)(2,1)S(1)} async-done(((bf16[32,64,128]{2,1,0:T(8,128)(2,1)}), bf16[32,64,128]{2,1,0:T(8,128)(2,1)S(1)}, u32[]{:S(2)}, u32[]{:S(2)}) %all-to-all-start.1) | async-done | bytes 524320 | tf_op jit(solution)/shard_map/all_to_all | solution.py:18
  53.4 0.1 convert_reduce_fusion
  53.5 0.2 convolution_convert_fusion
  53.7 0.0 copy-start.1
  53.7 34.8 %all_to_all.36.in_ref = bf16[32,32,128]{2,1,0:T(8,128)(2,1)S(1)} all-to-all(bf16[32,32,128]{2,1,0:T(8,128)(2,1)S(1)} %bitcast.44), channel_id=1, replica_groups=mesh['row'=32,'x'=4,'yhi'=4,'core'=2] {'row'}, dimensions={0} | all-to-all | bytes 524288 | tf_op jit(solution)/shard_map/all_to_all | solution.py:18
  88.5 1.1 shard_map.110
  89.6 7.9 %all-to-all-start.3 = ((bf16[32,128,128]{2,1,0:T(8,128)(2,1)}), bf16[32,128,128]{2,1,0:T(8,128)(2,1)S(1)}, u32[]{:S(2)}, u32[]{:S(2)}) async-start(bf16[32,128,128]{2,1,0:T(8,128)(2,1)} %shard_map.110), calls=%async_computation.3 | async-start | bytes 2097152 | tf_op jit(solution)/shard_map/all_to_all | solution.py:18
  97.5 2.1 collective-permute-start
  99.7 2.2 %collective-permute-start.1 = (bf16[4096,128]{1,0:T(8,128)(2,1)}, bf16[4096,128]{1,0:T(8,128)(2,1)}, u32[]{:S(2)}, u32[]{:S(2)}) collective-permute-start(bf16[4096,128]{1,0:T(8,128)(2,1)} %wu0_ref.1), channel_id=1, source_target_pairs={{0,1},{1,0},{2,3},{3,2},{4,5},{5,4},{6,7},{7,6},{8,9},{9,8},{10,11... | collective-permute-start | bytes 3145736 | tf_op jit(solution)/shard_map/ppermute | solution.py:22
  101.9 1.1 shard_map.112
  103.0 2.1 collective-permute-start.3
  105.2 0.0 collective-permute-done.wg1_ref
  105.2 21.1 %all-to-all-done.3.rows_ref = bf16[32,128,128]{2,1,0:T(8,128)(2,1)S(1)} async-done(((bf16[32,128,128]{2,1,0:T(8,128)(2,1)}), bf16[32,128,128]{2,1,0:T(8,128)(2,1)S(1)}, u32[]{:S(2)}, u32[]{:S(2)}) %all-to-all-start.3) | async-done | bytes 1048608 | tf_op jit(solution)/shard_map/all_to_all | solution.py:18
  126.3 1.2 copy-done.2
  127.5 1.2 copy-done.3
  128.8 2.3 %shard_map.111 = bf16[128,256]{1,0:T(8,128)(2,1)S(1)} custom-call(bf16[32,128,128]{2,1,0:T(8,128)(2,1)S(1)} %all-to-all-done.3.rows_ref, f32[16,256]{1,0:T(8,128)S(1)} %reshape.49.gain_ref, bf16[4096,128]{1,0:T(8,128)(2,1)S(1)} %copy-done.2, bf16[4096,128]{1,0:T(8,128)(2,1)} %collective-permute-done.wg1_ref, bf16[4096,128]{1,0:T(8,128)(2,1)S(1)} %copy-done.3, ...), custom_call_target="tpu_custom_call" | custom-call | tf_op jit(solution)/shard_map/pallas_call | solution.py:230
  131.1 0.7 broadcast_in_dim.22
  131.8 3.4 %all-to-all-start.4 = ((bf16[4,128,256]{2,1,0:T(8,128)(2,1)}), bf16[4,128,256]{2,1,0:T(8,128)(2,1)S(1)}, u32[]{:S(2)}, u32[]{:S(2)}) async-start(bf16[4,128,256]{2,1,0:T(8,128)(2,1)} %broadcast_in_dim.22), calls=%async_computation.4 | async-start | bytes 524288 | tf_op jit(solution)/shard_map/all_to_all | solution.py:18
  135.3 4.2 %collective-permute-start.4 = (bf16[2,128,512]{2,1,0:T(8,128)(2,1)S(1)}, bf16[2,128,512]{2,1,0:T(8,128)(2,1)S(1)}, u32[]{:S(2)}, u32[]{:S(2)}) collective-permute-start(bf16[2,128,512]{2,1,0:T(8,128)(2,1)S(1)} %pad_maximum_fusion.1), channel_id=1, source_target_pairs={{0,2},{2,4},{4,6},{6,0},{1,3},{3,5},{5,7},{7,1},{8,10},{10,12},{12... | collective-permute-start | bytes 786440 | tf_op jit(solution)/shard_map/ppermute | solution.py:26
  139.5 5.2 %collective-permute-start.5 = (bf16[2,128,512]{2,1,0:T(8,128)(2,1)S(1)}, bf16[2,128,512]{2,1,0:T(8,128)(2,1)S(1)}, u32[]{:S(2)}, u32[]{:S(2)}) collective-permute-start(bf16[2,128,512]{2,1,0:T(8,128)(2,1)S(1)} %pad_maximum_fusion.2), channel_id=1, source_target_pairs={{0,4},{2,6},{4,0},{6,2},{1,5},{3,7},{5,1},{7,3},{8,12},{10,14},{12... | collective-permute-start | bytes 786440 | tf_op jit(solution)/shard_map/ppermute | solution.py:26
  144.8 5.2 %collective-permute-start.6 = (bf16[2,128,512]{2,1,0:T(8,128)(2,1)S(1)}, bf16[2,128,512]{2,1,0:T(8,128)(2,1)S(1)}, u32[]{:S(2)}, u32[]{:S(2)}) collective-permute-start(bf16[2,128,512]{2,1,0:T(8,128)(2,1)S(1)} %pad_maximum_fusion.3), channel_id=1, source_target_pairs={{0,6},{2,0},{4,2},{6,4},{1,7},{3,1},{5,3},{7,5},{8,14},{10,8},{12,... | collective-permute-start | bytes 786440 | tf_op jit(solution)/shard_map/ppermute | solution.py:26
  150.0 4.5 %collective-permute-start.2 = (bf16[4,128,256]{2,1,0:T(8,128)(2,1)S(1)}, bf16[4,128,256]{2,1,0:T(8,128)(2,1)S(1)}, u32[]{:S(2)}, u32[]{:S(2)}) collective-permute-start(bf16[4,128,256]{2,1,0:T(8,128)(2,1)S(1)} %all-to-all-done.4.own_ref), channel_id=1, source_target_pairs={{0,1},{1,0},{2,3},{3,2},{4,5},{5,4},{6,7},{7,6},{8,9},{9,8},{10,11... | collective-permute-start | bytes 786440 | tf_op jit(solution)/shard_map/ppermute | solution.py:22
  154.5 0.1 eq.84
  154.6 0.1 fusion.10
  154.8 0.9 collective-permute-done.4.wd1_ref
  155.6 5.8 %collective-permute-done.5.wd2_ref = bf16[2,128,512]{2,1,0:T(8,128)(2,1)S(1)} collective-permute-done((bf16[2,128,512]{2,1,0:T(8,128)(2,1)S(1)}, bf16[2,128,512]{2,1,0:T(8,128)(2,1)S(1)}, u32[]{:S(2)}, u32[]{:S(2)}) %collective-permute-start.5) | collective-permute-done | bytes 262176 | tf_op jit(solution)/shard_map/ppermute | solution.py:26
  161.4 5.0 %collective-permute-done.6.wd3_ref = bf16[2,128,512]{2,1,0:T(8,128)(2,1)S(1)} collective-permute-done((bf16[2,128,512]{2,1,0:T(8,128)(2,1)S(1)}, bf16[2,128,512]{2,1,0:T(8,128)(2,1)S(1)}, u32[]{:S(2)}, u32[]{:S(2)}) %collective-permute-start.6) | collective-permute-done | bytes 262176 | tf_op jit(solution)/shard_map/ppermute | solution.py:26
  166.4 1.1 shard_map.113
  167.5 5.8 %all-to-all-start.5 = ((bf16[32,8,512]{2,1,0:T(8,128)(2,1)}), bf16[32,8,512]{2,1,0:T(8,128)(2,1)S(1)}, u32[]{:S(2)}, u32[]{:S(2)}) async-start(bf16[32,8,512]{2,1,0:T(8,128)(2,1)} %bitcast.10), calls=%async_computation.5 | async-start | bytes 524288 | tf_op jit(solution)/shard_map/all_to_all | solution.py:18
  173.3 0.1 compare_reduce_fusion
  173.4 0.1 fusion.19
  173.6 19.9 %all-to-all-done.5 = bf16[32,8,512]{2,1,0:T(8,128)(2,1)S(1)} async-done(((bf16[32,8,512]{2,1,0:T(8,128)(2,1)}), bf16[32,8,512]{2,1,0:T(8,128)(2,1)S(1)}, u32[]{:S(2)}, u32[]{:S(2)}) %all-to-all-start.5) | async-done | bytes 262176 | tf_op jit(solution)/shard_map/all_to_all | solution.py:18
  193.4 0.3 fusion.1
  193.8 20.4 %all_to_all.37.in_ref = bf16[32,2,512]{2,1,0:T(2,128)(2,1)S(1)} all-to-all(bf16[32,2,512]{2,1,0:T(2,128)(2,1)S(1)} %reshape.52), channel_id=1, replica_groups=mesh['row'=32,'x'=4,'yhi'=4,'core'=2] {'x','yhi','core'}, dimensions={0} | all-to-all | bytes 131072 | tf_op jit(solution)/shard_map/all_to_all | solution.py:18
  214.2 0.6 shard_map.114
  (32 shorter events, 0.4 us)
Async XLA Ops:
  0.0 37.6 %copy-start = (bf16[64,4096]{1,0:T(8,128)(2,1)S(1)}, bf16[64,4096]{1,0:T(8,128)(2,1)}, u32[]{:S(2)}) copy-start(bf16[64,4096]{1,0:T(8,128)(2,1)} %param.11) | copy-start | bytes 1572868
  1.4 35.9 %copy-start.4 = (s32[64,8]{0,1:T(8,128)S(1)}, s32[64,8]{0,1:T(8,128)}, u32[]{:S(2)}) copy-start(s32[64,8]{0,1:T(8,128)} %param.17) | copy-start | bytes 6148
  33.3 20.2 %all-to-all-start.1 = ((bf16[32,64,128]{2,1,0:T(8,128)(2,1)}), bf16[32,64,128]{2,1,0:T(8,128)(2,1)S(1)}, u32[]{:S(2)}, u32[]{:S(2)}) async-start(bf16[32,64,128]{2,1,0:T(8,128)(2,1)} %shard_map.109), calls=%async_computation.1 | async-start | bytes 1048576 | tf_op jit(solution)/shard_map/all_to_all | solution.py:18
  53.7 48.1 %copy-start.1 = (bf16[128,4096]{1,0:T(8,128)(2,1)S(1)}, bf16[128,4096]{1,0:T(8,128)(2,1)}, u32[]{:S(2)}) copy-start(bf16[128,4096]{1,0:T(8,128)(2,1)} %w_ref.3) | copy-start | bytes 3145732
  88.5 16.6 %copy-start.5 = (f32[4096]{0:T(1024)S(1)}, f32[4096]{0:T(1024)}, u32[]{:S(2)}) copy-start(f32[4096]{0:T(1024)} %param.16) | copy-start | bytes 49156
  88.5 16.6 %copy-start.6 = (f32[64,8]{0,1:T(8,128)S(1)}, f32[64,8]{0,1:T(8,128)}, u32[]{:S(2)}) copy-start(f32[64,8]{0,1:T(8,128)} %param.18) | copy-start | bytes 6148
  89.6 36.7 %all-to-all-start.3 = ((bf16[32,128,128]{2,1,0:T(8,128)(2,1)}), bf16[32,128,128]{2,1,0:T(8,128)(2,1)S(1)}, u32[]{:S(2)}, u32[]{:S(2)}) async-start(bf16[32,128,128]{2,1,0:T(8,128)(2,1)} %shard_map.110), calls=%async_computation.3 | async-start | bytes 2097152 | tf_op jit(solution)/shard_map/all_to_all | solution.py:18
  97.5 7.7 %collective-permute-start = (bf16[4096,128]{1,0:T(8,128)(2,1)}, bf16[4096,128]{1,0:T(8,128)(2,1)}, u32[]{:S(2)}, u32[]{:S(2)}) collective-permute-start(bf16[4096,128]{1,0:T(8,128)(2,1)} %wg0_ref.1), channel_id=1, source_target_pairs={{0,1},{1,0},{2,3},{3,2},{4,5},{5,4},{6,7},{7,6},{8,9},{9,8},{10,11... | collective-permute-start | bytes 3145736 | tf_op jit(solution)/shard_map/ppermute | solution.py:22
  99.7 5.5 %collective-permute-start.1 = (bf16[4096,128]{1,0:T(8,128)(2,1)}, bf16[4096,128]{1,0:T(8,128)(2,1)}, u32[]{:S(2)}, u32[]{:S(2)}) collective-permute-start(bf16[4096,128]{1,0:T(8,128)(2,1)} %wu0_ref.1), channel_id=1, source_target_pairs={{0,1},{1,0},{2,3},{3,2},{4,5},{5,4},{6,7},{7,6},{8,9},{9,8},{10,11... | collective-permute-start | bytes 3145736 | tf_op jit(solution)/shard_map/ppermute | solution.py:22
  103.0 32.2 %collective-permute-start.3 = (bf16[4,128,512]{2,1,0:T(8,128)(2,1)}, bf16[4,128,512]{2,1,0:T(8,128)(2,1)S(1)}, u32[]{:S(2)}, u32[]{:S(2)}) collective-permute-start(bf16[4,128,512]{2,1,0:T(8,128)(2,1)} %get-tuple-element.14), channel_id=1, source_target_pairs={{0,1},{1,0},{2,3},{3,2},{4,5},{5,4},{6,7},{7,6},{8,9},{9,8},{10,11... | collective-permute-start | bytes 1572872 | tf_op jit(solution)/shard_map/ppermute | solution.py:22
  126.3 1.2 copy-start.2
  127.5 1.2 copy-start.3
  131.8 18.2 %all-to-all-start.4 = ((bf16[4,128,256]{2,1,0:T(8,128)(2,1)}), bf16[4,128,256]{2,1,0:T(8,128)(2,1)S(1)}, u32[]{:S(2)}, u32[]{:S(2)}) async-start(bf16[4,128,256]{2,1,0:T(8,128)(2,1)} %broadcast_in_dim.22), calls=%async_computation.4 | async-start | bytes 524288 | tf_op jit(solution)/shard_map/all_to_all | solution.py:18
  135.3 20.4 %collective-permute-start.4 = (bf16[2,128,512]{2,1,0:T(8,128)(2,1)S(1)}, bf16[2,128,512]{2,1,0:T(8,128)(2,1)S(1)}, u32[]{:S(2)}, u32[]{:S(2)}) collective-permute-start(bf16[2,128,512]{2,1,0:T(8,128)(2,1)S(1)} %pad_maximum_fusion.1), channel_id=1, source_target_pairs={{0,2},{2,4},{4,6},{6,0},{1,3},{3,5},{5,7},{7,1},{8,10},{10,12},{12... | collective-permute-start | bytes 786440 | tf_op jit(solution)/shard_map/ppermute | solution.py:26
  139.5 21.9 %collective-permute-start.5 = (bf16[2,128,512]{2,1,0:T(8,128)(2,1)S(1)}, bf16[2,128,512]{2,1,0:T(8,128)(2,1)S(1)}, u32[]{:S(2)}, u32[]{:S(2)}) collective-permute-start(bf16[2,128,512]{2,1,0:T(8,128)(2,1)S(1)} %pad_maximum_fusion.2), channel_id=1, source_target_pairs={{0,4},{2,6},{4,0},{6,2},{1,5},{3,7},{5,1},{7,3},{8,12},{10,14},{12... | collective-permute-start | bytes 786440 | tf_op jit(solution)/shard_map/ppermute | solution.py:26
  144.8 21.6 %collective-permute-start.6 = (bf16[2,128,512]{2,1,0:T(8,128)(2,1)S(1)}, bf16[2,128,512]{2,1,0:T(8,128)(2,1)S(1)}, u32[]{:S(2)}, u32[]{:S(2)}) collective-permute-start(bf16[2,128,512]{2,1,0:T(8,128)(2,1)S(1)} %pad_maximum_fusion.3), channel_id=1, source_target_pairs={{0,6},{2,0},{4,2},{6,4},{1,7},{3,1},{5,3},{7,5},{8,14},{10,8},{12,... | collective-permute-start | bytes 786440 | tf_op jit(solution)/shard_map/ppermute | solution.py:26
  150.0 16.4 %collective-permute-start.2 = (bf16[4,128,256]{2,1,0:T(8,128)(2,1)S(1)}, bf16[4,128,256]{2,1,0:T(8,128)(2,1)S(1)}, u32[]{:S(2)}, u32[]{:S(2)}) collective-permute-start(bf16[4,128,256]{2,1,0:T(8,128)(2,1)S(1)} %all-to-all-done.4.own_ref), channel_id=1, source_target_pairs={{0,1},{1,0},{2,3},{3,2},{4,5},{5,4},{6,7},{7,6},{8,9},{9,8},{10,11... | collective-permute-start | bytes 786440 | tf_op jit(solution)/shard_map/ppermute | solution.py:22
  167.5 25.9 %all-to-all-start.5 = ((bf16[32,8,512]{2,1,0:T(8,128)(2,1)}), bf16[32,8,512]{2,1,0:T(8,128)(2,1)S(1)}, u32[]{:S(2)}, u32[]{:S(2)}) async-start(bf16[32,8,512]{2,1,0:T(8,128)(2,1)} %bitcast.10), calls=%async_computation.5 | async-start | bytes 524288 | tf_op jit(solution)/shard_map/all_to_all | solution.py:18
